TPU v7x, 32 devices: a whole 2x2x4 slice. The times are simulated.
32 devices in a mesh: tm: 8 (over z, y), space: 4 (over x, core).
Axes of the slice: x: 2, y: 2, z: 4, core: 2. Of those that a mesh axis runs over, the one named last changes fastest.
Arguments:
- start_values: float32 [8, 2, 1024, 1024], P('tm', None, 'space'), may hold values from -6 to 6
- node_values: float32 [8, 2, 2, 1024, 1024], P('tm', None, None, 'space'), may hold values from -6 to 6
Outputs:
- next_start: float32 [8, 2, 1024, 1024], P('tm', None, 'space')
- next_nodes: float32 [8, 2, 2, 1024, 1024], P('tm', None, None, 'space')
All inputs are finite; a program needn't handle non-finite values.
Results may differ from a plain program's by a relative error of at most 0.00002.
Values sent between devices are 32-bit elements; how exact they have to be, the bound alone decides.
A program may use at most 64 MiB of HBM per device.

v0:
```python
import jax
import jax.numpy as jnp
from jax import lax
from jax.sharding import PartitionSpec as P

KX = 1024
KY = 1024
CX = 256


diffusion = 1.5
drift = 0.8
shear = 0.6
first_weights = (5.0 / 24.0, 1.0 / 3.0, -1.0 / 24.0)
second_weights = (-1.0 / 24.0, 1.0 / 3.0, 5.0 / 24.0)
whole_weights = (1.0 / 6.0, 2.0 / 3.0, 1.0 / 6.0)


def with_halo(shard, sides, width):
    for axis, dim in sides:
        peers, length = (lax.axis_size(axis), shard.shape[dim])
        up = [(i, (i + 1) % peers) for i in range(peers - 1)]
        down = [(j, i) for i, j in up]
        last = lax.slice_in_dim(shard, length - width, length, axis=dim)
        first = lax.slice_in_dim(shard, 0, width, axis=dim)
        before = lax.ppermute(last, axis, up)
        after = lax.ppermute(first, axis, down)
        shard = jnp.concatenate([before, shard, after], axis=dim)
    return shard


def from_behind(value, axis, steps):
    count = lax.axis_size(axis)
    first, last = (max(0, -steps), min(count, count - steps))
    return lax.ppermute(value, axis, [(source, source + steps) for source in range(first, last)])


def spectrum(row_index, column_index):
    along = (row_index.astype(jnp.float32) - KX // 2) / (KX // 2)
    across = (column_index.astype(jnp.float32) - KY // 2) / (KY // 2)
    real_rate = -diffusion * (along[:, None] * along[:, None] + across[None, :] * across[None, :])
    imag_rate = -drift * across[None, :] + 0.0 * along[:, None]
    return (real_rate, imag_rate, across)


def multiply(real_rate, imag_rate, field):
    return jnp.stack(
        [
            real_rate * field[..., 0, :, :] - imag_rate * field[..., 1, :, :],
            real_rate * field[..., 1, :, :] + imag_rate * field[..., 0, :, :],
        ],
        axis=-3,
    )


def divide(real_part, imag_part, field):
    modulus = real_part * real_part + imag_part * imag_part
    return jnp.stack(
        [
            (field[..., 0, :, :] * real_part + field[..., 1, :, :] * imag_part) / modulus,
            (field[..., 1, :, :] * real_part - field[..., 0, :, :] * imag_part) / modulus,
        ],
        axis=-3,
    )


def explicit(field, across):
    padded = with_halo(field, (("space", 2),), 1)
    sums = padded[..., 2:, :] + padded[..., :-2, :]
    factor = shear * across
    return jnp.stack([factor * sums[..., 1, :, :], -factor * sums[..., 0, :, :]], axis=-3)


def body(start_values, node_values):
    begin_value = start_values[0]
    old_nodes = node_values[0]
    slab_rows = begin_value.shape[1]
    slab_columns = begin_value.shape[2]
    leader = lax.axis_index("tm") == 0
    rank = lax.axis_index("space")
    row_index = rank * slab_rows + lax.iota(jnp.int32, slab_rows)
    real_rate, imag_rate, across = spectrum(row_index, lax.iota(jnp.int32, slab_columns))
    stacked = jnp.stack([begin_value, old_nodes[0], old_nodes[1]])
    old_coupling = explicit(stacked, across)
    old_slopes = multiply(real_rate, imag_rate, stacked) + old_coupling
    sum_one = (
        first_weights[0] * old_slopes[0]
        + first_weights[1] * old_slopes[1]
        + first_weights[2] * old_slopes[2]
    )
    sum_two = (
        second_weights[0] * old_slopes[0]
        + second_weights[1] * old_slopes[1]
        + second_weights[2] * old_slopes[2]
    )
    half_real = 1.0 - 0.5 * real_rate
    half_imag = -0.5 * imag_rate
    node_one = divide(
        half_real,
        half_imag,
        begin_value - 0.5 * multiply(real_rate, imag_rate, old_nodes[0]) + sum_one,
    )
    one_coupling = explicit(node_one[None], across)[0]
    node_two = divide(
        half_real,
        half_imag,
        node_one
        + 0.5 * (one_coupling - old_coupling[1])
        - 0.5 * multiply(real_rate, imag_rate, old_nodes[1])
        + sum_two,
    )
    two_coupling = explicit(node_two[None], across)[0]
    integral = (
        whole_weights[0] * old_slopes[0]
        + whole_weights[1] * (multiply(real_rate, imag_rate, node_one) + one_coupling)
        + whole_weights[2] * (multiply(real_rate, imag_rate, node_two) + two_coupling)
    )
    low_row = KX // 2 - CX // 2
    low_column = KY // 2 - CX // 2
    row_mask = ((row_index >= low_row) & (row_index < low_row + CX)).astype(jnp.float32)[:, None]

    def restrict(field):
        return field[..., low_column : low_column + CX] * row_mask

    def enlarge(field):
        return jnp.pad(field, ((0, 0), (0, 0), (low_column, slab_columns - low_column - CX)))

    coarse_real = real_rate[:, low_column : low_column + CX]
    coarse_imag = imag_rate[:, low_column : low_column + CX]
    begin_coarse = restrict(begin_value)
    end_coarse = restrict(node_two)
    tau = restrict(integral) - 0.5 * multiply(coarse_real, coarse_imag, begin_coarse + end_coarse)
    offset = 0.5 * multiply(coarse_real, coarse_imag, begin_coarse - end_coarse) + tau
    step_real = 1.0 - coarse_real
    step_imag = -coarse_imag

    def relay(counter, begin_now):
        finish = divide(step_real, step_imag, begin_now + offset)
        incoming = from_behind(finish, "tm", 1)
        return jnp.where(leader, begin_coarse, incoming)

    begin_new = lax.fori_loop(0, lax.axis_size("tm") - 1, relay, begin_coarse)
    end_new = divide(step_real, step_imag, begin_new + offset)
    delta_begin = begin_new - begin_coarse
    delta_end = end_new - end_coarse
    fixed_one = node_one + enlarge(0.5 * (delta_begin + delta_end))
    fixed_two = node_two + enlarge(delta_end)
    arrived = from_behind(fixed_two, "tm", 1)
    next_start = jnp.where(leader, begin_value, arrived)
    next_nodes = jnp.stack([fixed_one, fixed_two])
    return (next_start[None], next_nodes[None])


def solution(mesh):
    in_specs = (P("tm", None, "space", None), P("tm", None, None, "space", None))
    out_specs = (P("tm", None, "space", None), P("tm", None, None, "space", None))
    return jax.shard_map(body, mesh=mesh, in_specs=in_specs, out_specs=out_specs, check_vma=False)
```

profile of v0, /device:TPU:8, one launch (start us, length us, event | category | flops | bytes accessed | tf_op | source)
XLA Modules:
  0.0 233.1 jit_solution(17927046781905600992)
XLA Ops:
  0.6 2.7 %slice_bitcast_fusion.1 = (f32[1,2,256,1024]{3,2,1,0:T(8,128)S(1)}, f32[1,2,256,1024]{3,2,1,0:T(8,128)S(1)}) fusion(f32[1,2,2,256,1024]{4,3,2,1,0:T(8,128)} %param.5), kind=kLoop, calls=%fused_computation.70 | loop fusion | bytes 8388608 | tf_op jit(solution)/shard_map/slice | solution.py:101
  3.5 1.1 copy-done.9
  5.3 1.7 collective-permute-start.2
  7.1 1.3 collective-permute-start.1
  8.4 1.1 broadcast_add_fusion
  9.6 5.0 %fusion.32 = (f32[1,256,1024]{2,1,0:T(8,128)}, f32[1,256,1024]{2,1,0:T(8,128)}, f32[1,256,1024]{2,1,0:T(8,128)}, f32[1,256,1024]{2,1,0:T(8,128)}) fusion(f32[1,2,2,256,1024]{4,3,2,1,0:T(8,128)} %param.5, f32[256]{0:T(256)S(1)} %get-tuple-element.187, f32[1024]{0:T(1024)S(1)} %get-tuple-element.191, f32[1024]{0:T(1024)S(1)} %get-tuple-element.190, ...), kind=kLoop, calls=%fused_computation.83 | loop fusion | flops 3932160 | bytes 8398848 | tf_op jit(solution)/shard_map/sub | solution.py:49
  14.8 7.6 %pad_maximum_fusion.8 = (f32[3,2,256,1024]{3,2,1,0:T(8,128)S(1)}, f32[3,2,256,1024]{3,2,1,0:T(8,128)S(1)}) fusion(f32[1,2,256,1024]{3,2,1,0:T(8,128)} %copy-done.10, f32[1,2,256,1024]{3,2,1,0:T(8,128)} %copy-done.9, f32[1,2,256,1024]{3,2,1,0:T(8,128)S(1)} %copy-done, f32[3,2,1,1024]{3,2,1,0:T(1,128)S(1)} %collective-permute-done.2, ...), kind=kLoop, calls=%fused_computation.21 | loop fusion | flops 14155776 | bytes 18923520 | tf_op jit(solution)/shard_map/stack | solution.py:83
  22.5 1.8 multiply_subtract_fusion
  25.0 1.4 fusion.4
  26.5 1.3 fusion.21
  29.0 4.3 %collective-permute-start.4 = (f32[1,2,1,1024]{3,2,1,0:T(1,128)S(1)}, f32[1,2,1,1024]{3,2,1,0:T(1,128)S(1)}, u32[]{:S(2)}, u32[]{:S(2)}) collective-permute-start(f32[1,2,1,1024]{3,2,1,0:T(1,128)S(1)} %get-tuple-element.182), channel_id=1, source_target_pairs={{0,1},{1,2},{2,3},{4,5},{5,6},{6,7},{8,9},{9,10},{10,11},{12,13},{... | collective-permute-start | bytes 24584 | tf_op jit(solution)/shard_map/ppermute | solution.py:26
  33.3 1.3 collective-permute-start.3
  35.0 2.6 %collective-permute-done.3 = f32[1,2,1,1024]{3,2,1,0:T(1,128)S(1)} collective-permute-done((f32[1,2,1,1024]{3,2,1,0:T(1,128)S(1)}, f32[1,2,1,1024]{3,2,1,0:T(1,128)S(1)}, u32[]{:S(2)}, u32[]{:S(2)}) %collective-permute-start.3) | collective-permute-done | bytes 8224 | tf_op jit(solution)/shard_map/ppermute | solution.py:27
  39.5 1.7 fusion.17
  43.0 4.3 %collective-permute-start.6 = (f32[1,2,1,1024]{3,2,1,0:T(1,128)S(1)}, f32[1,2,1,1024]{3,2,1,0:T(1,128)S(1)}, u32[]{:S(2)}, u32[]{:S(2)}) collective-permute-start(f32[1,2,1,1024]{3,2,1,0:T(1,128)S(1)} %get-tuple-element.178), channel_id=1, source_target_pairs={{0,1},{1,2},{2,3},{4,5},{5,6},{6,7},{8,9},{9,10},{10,11},{12,13},{... | collective-permute-start | bytes 24584 | tf_op jit(solution)/shard_map/ppermute | solution.py:26
  47.3 1.5 collective-permute-start.5
  49.0 2.0 subtract_bitcast_fusion
  52.1 1.1 fusion.60
  53.3 129.6 %while.13 = (s32[]{:T(128)}, f32[2,256,256]{2,1,0:T(8,128)S(1)}, pred[]{:T(512)}, f32[2,256,256]{2,1,0:T(8,128)}, f32[256,256]{1,0:T(8,128)S(1)}, /*index=5*/f32...) while((s32[]{:T(128)}, f32[2,256,256]{2,1,0:T(8,128)S(1)}, pred[]{:T(512)}, ...), condition=%wide.region_1.2_spmd, body=%wide.region_0.1_spmd.sunk | while | flops 917506 | bytes 8126598 | solution.py:142
  54.4 1.1 fusion.78
  55.6 3.4 %collective-permute-start = (f32[2,256,256]{2,1,0:T(8,128)S(1)}, f32[2,256,256]{2,1,0:T(8,128)}, u32[]{:S(2)}, u32[]{:S(2)}) collective-permute-start(f32[2,256,256]{2,1,0:T(8,128)S(1)} %pad_maximum_fusion.20), channel_id=1, source_target_pairs={{0,4},{4,8},{8,12},{12,16},{16,20},{20,24},{24,28},{1,5},{5,9},{9,... | collective-permute-start | bytes 1572872 | tf_op jit(solution)/shard_map/while/body/eval_jaxpr/ppermute | solution.py:35
  59.0 14.1 %collective-permute-done = f32[2,256,256]{2,1,0:T(8,128)} collective-permute-done((f32[2,256,256]{2,1,0:T(8,128)S(1)}, f32[2,256,256]{2,1,0:T(8,128)}, u32[]{:S(2)}, u32[]{:S(2)}) %collective-permute-start) | collective-permute-done | bytes 524320 | tf_op jit(solution)/shard_map/while/body/eval_jaxpr/ppermute | solution.py:35
  74.2 1.1 add.686
  75.3 1.1 fusion.78
  76.5 2.5 %collective-permute-start = (f32[2,256,256]{2,1,0:T(8,128)S(1)}, f32[2,256,256]{2,1,0:T(8,128)}, u32[]{:S(2)}, u32[]{:S(2)}) collective-permute-start(f32[2,256,256]{2,1,0:T(8,128)S(1)} %pad_maximum_fusion.20), channel_id=1, source_target_pairs={{0,4},{4,8},{8,12},{12,16},{16,20},{20,24},{24,28},{1,5},{5,9},{9,... | collective-permute-start | bytes 1572872 | tf_op jit(solution)/shard_map/while/body/eval_jaxpr/ppermute | solution.py:35
  79.0 14.3 %collective-permute-done = f32[2,256,256]{2,1,0:T(8,128)} collective-permute-done((f32[2,256,256]{2,1,0:T(8,128)S(1)}, f32[2,256,256]{2,1,0:T(8,128)}, u32[]{:S(2)}, u32[]{:S(2)}) %collective-permute-start) | collective-permute-done | bytes 524320 | tf_op jit(solution)/shard_map/while/body/eval_jaxpr/ppermute | solution.py:35
  94.5 1.1 add.686
  95.6 1.1 fusion.78
  96.8 1.9 collective-permute-start
  98.7 14.1 %collective-permute-done = f32[2,256,256]{2,1,0:T(8,128)} collective-permute-done((f32[2,256,256]{2,1,0:T(8,128)S(1)}, f32[2,256,256]{2,1,0:T(8,128)}, u32[]{:S(2)}, u32[]{:S(2)}) %collective-permute-start) | collective-permute-done | bytes 524320 | tf_op jit(solution)/shard_map/while/body/eval_jaxpr/ppermute | solution.py:35
  115.0 1.1 fusion.78
  116.2 1.9 collective-permute-start
  118.1 13.2 %collective-permute-done = f32[2,256,256]{2,1,0:T(8,128)} collective-permute-done((f32[2,256,256]{2,1,0:T(8,128)S(1)}, f32[2,256,256]{2,1,0:T(8,128)}, u32[]{:S(2)}, u32[]{:S(2)}) %collective-permute-start) | collective-permute-done | bytes 524320 | tf_op jit(solution)/shard_map/while/body/eval_jaxpr/ppermute | solution.py:35
  133.5 1.1 fusion.78
  134.7 1.9 collective-permute-start
  136.6 12.3 %collective-permute-done = f32[2,256,256]{2,1,0:T(8,128)} collective-permute-done((f32[2,256,256]{2,1,0:T(8,128)S(1)}, f32[2,256,256]{2,1,0:T(8,128)}, u32[]{:S(2)}, u32[]{:S(2)}) %collective-permute-start) | collective-permute-done | bytes 524320 | tf_op jit(solution)/shard_map/while/body/eval_jaxpr/ppermute | solution.py:35
  151.2 1.1 fusion.78
  152.4 1.9 collective-permute-start
  154.3 11.5 %collective-permute-done = f32[2,256,256]{2,1,0:T(8,128)} collective-permute-done((f32[2,256,256]{2,1,0:T(8,128)S(1)}, f32[2,256,256]{2,1,0:T(8,128)}, u32[]{:S(2)}, u32[]{:S(2)}) %collective-permute-start) | collective-permute-done | bytes 524320 | tf_op jit(solution)/shard_map/while/body/eval_jaxpr/ppermute | solution.py:35
  168.0 1.1 fusion.78
  169.2 1.9 collective-permute-start
  171.1 10.6 %collective-permute-done = f32[2,256,256]{2,1,0:T(8,128)} collective-permute-done((f32[2,256,256]{2,1,0:T(8,128)S(1)}, f32[2,256,256]{2,1,0:T(8,128)}, u32[]{:S(2)}, u32[]{:S(2)}) %collective-permute-start) | collective-permute-done | bytes 524320 | tf_op jit(solution)/shard_map/while/body/eval_jaxpr/ppermute | solution.py:35
  182.9 1.2 add.374
  184.1 1.3 divide_bitcast_fusion.1
  186.0 2.1 collective-permute-start.7
  188.5 2.3 maximum_bitcast_fusion
  190.8 40.6 %collective-permute-done.7 = f32[2,256,1024]{2,1,0:T(8,128)S(1)} collective-permute-done((f32[2,256,1024]{2,1,0:T(8,128)S(1)}, f32[2,256,1024]{2,1,0:T(8,128)S(1)}, u32[]{:S(2)}, u32[]{:S(2)}) %collective-permute-start.7) | collective-permute-done | bytes 2097184 | tf_op jit(solution)/shard_map/ppermute | solution.py:35
  231.4 1.7 select_bitcast_fusion
  (90 shorter events, 22.8 us)
Async XLA Ops:
  0.6 2.9 %copy-start = (f32[1,2,256,1024]{3,2,1,0:T(8,128)S(1)}, f32[1,2,256,1024]{3,2,1,0:T(8,128)}, u32[]{:S(2)}) copy-start(f32[1,2,256,1024]{3,2,1,0:T(8,128)} %param.4) | copy-start | bytes 6291460
  3.3 1.3 copy-start.9
  3.3 2.0 copy-start.10
  5.3 9.5 %collective-permute-start.2 = (f32[3,2,1,1024]{3,2,1,0:T(1,128)S(1)}, f32[3,2,1,1024]{3,2,1,0:T(1,128)S(1)}, u32[]{:S(2)}, u32[]{:S(2)}) collective-permute-start(f32[3,2,1,1024]{3,2,1,0:T(1,128)S(1)} %get-tuple-element.159), channel_id=1, source_target_pairs={{0,1},{1,2},{2,3},{4,5},{5,6},{6,7},{8,9},{9,10},{10,11},{12,13},{... | collective-permute-start | bytes 73736 | tf_op jit(solution)/shard_map/ppermute | solution.py:26
  7.1 7.7 %collective-permute-start.1 = (f32[3,2,1,1024]{3,2,1,0:T(1,128)S(1)}, f32[3,2,1,1024]{3,2,1,0:T(1,128)S(1)}, u32[]{:S(2)}, u32[]{:S(2)}) collective-permute-start(f32[3,2,1,1024]{3,2,1,0:T(1,128)S(1)} %get-tuple-element.158), channel_id=1, source_target_pairs={{1,0},{2,1},{3,2},{5,4},{6,5},{7,6},{9,8},{10,9},{11,10},{13,12},{... | collective-permute-start | bytes 73736 | tf_op jit(solution)/shard_map/ppermute | solution.py:27
  14.7 7.7 %copy-start.11 = (f32[256,1024]{1,0:T(8,128)}, f32[256,1024]{1,0:T(8,128)S(1)}, u32[]{:S(2)}) copy-start(f32[256,1024]{1,0:T(8,128)S(1)} %add_multiply_fusion.11) | copy-start | bytes 3145732
  14.8 7.7 %copy-start.12 = (f32[256,1024]{1,0:T(8,128)S(1)}, f32[256,1024]{1,0:T(8,128)}, u32[]{:S(2)}) copy-start(f32[256,1024]{1,0:T(8,128)} %broadcast_add_fusion) | copy-start | bytes 3145732
  25.0 1.4 copy-start.17
  25.0 1.5 copy-start.18
  28.7 13.7 %copy-start.5 = (f32[1,256,1024]{2,1,0:T(8,128)}, f32[1,256,1024]{2,1,0:T(8,128)S(1)}, u32[]{:S(2)}) copy-start(f32[1,256,1024]{2,1,0:T(8,128)S(1)} %get-tuple-element.145) | copy-start | bytes 3145732
  28.7 13.7 %copy-start.7 = (f32[1,256,1024]{2,1,0:T(8,128)}, f32[1,256,1024]{2,1,0:T(8,128)S(1)}, u32[]{:S(2)}) copy-start(f32[1,256,1024]{2,1,0:T(8,128)S(1)} %get-tuple-element.146) | copy-start | bytes 3145732
  29.0 6.0 %collective-permute-start.4 = (f32[1,2,1,1024]{3,2,1,0:T(1,128)S(1)}, f32[1,2,1,1024]{3,2,1,0:T(1,128)S(1)}, u32[]{:S(2)}, u32[]{:S(2)}) collective-permute-start(f32[1,2,1,1024]{3,2,1,0:T(1,128)S(1)} %get-tuple-element.182), channel_id=1, source_target_pairs={{0,1},{1,2},{2,3},{4,5},{5,6},{6,7},{8,9},{9,10},{10,11},{12,13},{... | collective-permute-start | bytes 24584 | tf_op jit(solution)/shard_map/ppermute | solution.py:26
  33.3 4.3 %collective-permute-start.3 = (f32[1,2,1,1024]{3,2,1,0:T(1,128)S(1)}, f32[1,2,1,1024]{3,2,1,0:T(1,128)S(1)}, u32[]{:S(2)}, u32[]{:S(2)}) collective-permute-start(f32[1,2,1,1024]{3,2,1,0:T(1,128)S(1)} %get-tuple-element.181), channel_id=1, source_target_pairs={{1,0},{2,1},{3,2},{5,4},{6,5},{7,6},{9,8},{10,9},{11,10},{13,12},{... | collective-permute-start | bytes 24584 | tf_op jit(solution)/shard_map/ppermute | solution.py:27
  38.0 1.2 copy-start.15
  38.0 1.5 copy-start.16
  42.2 6.6 %copy-start.1 = (f32[1,256,1024]{2,1,0:T(8,128)}, f32[1,256,1024]{2,1,0:T(8,128)S(1)}, u32[]{:S(2)}) copy-start(f32[1,256,1024]{2,1,0:T(8,128)S(1)} %get-tuple-element.148) | copy-start | bytes 3145732
  42.2 6.6 %copy-start.3 = (f32[1,256,1024]{2,1,0:T(8,128)}, f32[1,256,1024]{2,1,0:T(8,128)S(1)}, u32[]{:S(2)}) copy-start(f32[1,256,1024]{2,1,0:T(8,128)S(1)} %get-tuple-element.149) | copy-start | bytes 3145732
  43.0 8.4 %collective-permute-start.6 = (f32[1,2,1,1024]{3,2,1,0:T(1,128)S(1)}, f32[1,2,1,1024]{3,2,1,0:T(1,128)S(1)}, u32[]{:S(2)}, u32[]{:S(2)}) collective-permute-start(f32[1,2,1,1024]{3,2,1,0:T(1,128)S(1)} %get-tuple-element.178), channel_id=1, source_target_pairs={{0,1},{1,2},{2,3},{4,5},{5,6},{6,7},{8,9},{9,10},{10,11},{12,13},{... | collective-permute-start | bytes 24584 | tf_op jit(solution)/shard_map/ppermute | solution.py:26
  47.3 4.1 %collective-permute-start.5 = (f32[1,2,1,1024]{3,2,1,0:T(1,128)S(1)}, f32[1,2,1,1024]{3,2,1,0:T(1,128)S(1)}, u32[]{:S(2)}, u32[]{:S(2)}) collective-permute-start(f32[1,2,1,1024]{3,2,1,0:T(1,128)S(1)} %get-tuple-element.177), channel_id=1, source_target_pairs={{1,0},{2,1},{3,2},{5,4},{6,5},{7,6},{9,8},{10,9},{11,10},{13,12},{... | collective-permute-start | bytes 24584 | tf_op jit(solution)/shard_map/ppermute | solution.py:27
  49.0 2.1 copy-start.13
  55.6 17.5 %collective-permute-start = (f32[2,256,256]{2,1,0:T(8,128)S(1)}, f32[2,256,256]{2,1,0:T(8,128)}, u32[]{:S(2)}, u32[]{:S(2)}) collective-permute-start(f32[2,256,256]{2,1,0:T(8,128)S(1)} %pad_maximum_fusion.20), channel_id=1, source_target_pairs={{0,4},{4,8},{8,12},{12,16},{16,20},{20,24},{24,28},{1,5},{5,9},{9,... | collective-permute-start | bytes 1572872 | tf_op jit(solution)/shard_map/while/body/eval_jaxpr/ppermute | solution.py:35
  76.5 16.8 %collective-permute-start = (f32[2,256,256]{2,1,0:T(8,128)S(1)}, f32[2,256,256]{2,1,0:T(8,128)}, u32[]{:S(2)}, u32[]{:S(2)}) collective-permute-start(f32[2,256,256]{2,1,0:T(8,128)S(1)} %pad_maximum_fusion.20), channel_id=1, source_target_pairs={{0,4},{4,8},{8,12},{12,16},{16,20},{20,24},{24,28},{1,5},{5,9},{9,... | collective-permute-start | bytes 1572872 | tf_op jit(solution)/shard_map/while/body/eval_jaxpr/ppermute | solution.py:35
  96.8 16.0 %collective-permute-start = (f32[2,256,256]{2,1,0:T(8,128)S(1)}, f32[2,256,256]{2,1,0:T(8,128)}, u32[]{:S(2)}, u32[]{:S(2)}) collective-permute-start(f32[2,256,256]{2,1,0:T(8,128)S(1)} %pad_maximum_fusion.20), channel_id=1, source_target_pairs={{0,4},{4,8},{8,12},{12,16},{16,20},{20,24},{24,28},{1,5},{5,9},{9,... | collective-permute-start | bytes 1572872 | tf_op jit(solution)/shard_map/while/body/eval_jaxpr/ppermute | solution.py:35
  116.2 15.1 %collective-permute-start = (f32[2,256,256]{2,1,0:T(8,128)S(1)}, f32[2,256,256]{2,1,0:T(8,128)}, u32[]{:S(2)}, u32[]{:S(2)}) collective-permute-start(f32[2,256,256]{2,1,0:T(8,128)S(1)} %pad_maximum_fusion.20), channel_id=1, source_target_pairs={{0,4},{4,8},{8,12},{12,16},{16,20},{20,24},{24,28},{1,5},{5,9},{9,... | collective-permute-start | bytes 1572872 | tf_op jit(solution)/shard_map/while/body/eval_jaxpr/ppermute | solution.py:35
  134.7 14.3 %collective-permute-start = (f32[2,256,256]{2,1,0:T(8,128)S(1)}, f32[2,256,256]{2,1,0:T(8,128)}, u32[]{:S(2)}, u32[]{:S(2)}) collective-permute-start(f32[2,256,256]{2,1,0:T(8,128)S(1)} %pad_maximum_fusion.20), channel_id=1, source_target_pairs={{0,4},{4,8},{8,12},{12,16},{16,20},{20,24},{24,28},{1,5},{5,9},{9,... | collective-permute-start | bytes 1572872 | tf_op jit(solution)/shard_map/while/body/eval_jaxpr/ppermute | solution.py:35
  152.4 13.4 %collective-permute-start = (f32[2,256,256]{2,1,0:T(8,128)S(1)}, f32[2,256,256]{2,1,0:T(8,128)}, u32[]{:S(2)}, u32[]{:S(2)}) collective-permute-start(f32[2,256,256]{2,1,0:T(8,128)S(1)} %pad_maximum_fusion.20), channel_id=1, source_target_pairs={{0,4},{4,8},{8,12},{12,16},{16,20},{20,24},{24,28},{1,5},{5,9},{9,... | collective-permute-start | bytes 1572872 | tf_op jit(solution)/shard_map/while/body/eval_jaxpr/ppermute | solution.py:35
  169.2 12.6 %collective-permute-start = (f32[2,256,256]{2,1,0:T(8,128)S(1)}, f32[2,256,256]{2,1,0:T(8,128)}, u32[]{:S(2)}, u32[]{:S(2)}) collective-permute-start(f32[2,256,256]{2,1,0:T(8,128)S(1)} %pad_maximum_fusion.20), channel_id=1, source_target_pairs={{0,4},{4,8},{8,12},{12,16},{16,20},{20,24},{24,28},{1,5},{5,9},{9,... | collective-permute-start | bytes 1572872 | tf_op jit(solution)/shard_map/while/body/eval_jaxpr/ppermute | solution.py:35
  182.9 2.5 %copy-start.14 = (f32[2,256,256]{2,1,0:T(8,128)S(1)}, f32[2,256,256]{2,1,0:T(8,128)}, u32[]{:S(2)}) copy-start(f32[2,256,256]{2,1,0:T(8,128)} %copy-done.13) | copy-start | bytes 1572868
  184.1 1.5 copy-start.2
  184.1 1.7 copy-start.4
  186.0 2.3 copy-start.6
  186.0 2.3 copy-start.8
  186.0 45.4 %collective-permute-start.7 = (f32[2,256,1024]{2,1,0:T(8,128)S(1)}, f32[2,256,1024]{2,1,0:T(8,128)S(1)}, u32[]{:S(2)}, u32[]{:S(2)}) collective-permute-start(f32[2,256,1024]{2,1,0:T(8,128)S(1)} %pad_add_fusion), channel_id=1, source_target_pairs={{0,4},{4,8},{8,12},{12,16},{16,20},{20,24},{24,28},{1,5},{5,9},{9,... | collective-permute-start | bytes 6291464 | tf_op jit(solution)/shard_map/ppermute | solution.py:35
where the time goes:
time: 235 us; the launch traced here: 233 us
  waiting for transfers between devices  133 us (57%)
  other arithmetic  59.9 us (25%)
  starting transfers between devices  32 us (14%)
  local copies, waits for them, and re-layouts  6.28 us (3%)
    ppermute x8, waiting for transfers between devices, from_behind(): lax.ppermute(value, axis, [(source, source + steps) for source in range(f...  131 us
    ppermute x8, starting transfers between devices, from_behind(): lax.ppermute(value, axis, [(source, source + steps) for source in range(f...  17.6 us
    ppermute x3, starting transfers between devices, with_halo(): before = lax.ppermute(last, axis, up)  10.3 us
    sub x4, other arithmetic, multiply(): real_rate * field[..., 0, :, :] - imag_rate * field[..., 1, :, :]  8.57 us
    div x7, other arithmetic, divide(): (field[..., 0, :, :] * real_part + field[..., 1, :, :] * imag_part) / mod...  7.85 us
    add x7, other arithmetic, relay(): finish = divide(step_real, step_imag, begin_now + offset)  7.77 us
    select_n x7, other arithmetic, relay(): return jnp.where(leader, begin_coarse, incoming)  7.77 us
    another operation x1, other arithmetic, body(): stacked = jnp.stack([begin_value, old_nodes[0], old_nodes[1]])  7.62 us
  transfers between devices with their start and end apart: 14, of which 9 were waited for; matrix products, arithmetic and copies ran while one was open for 5% of the time, Pallas kernels for 0%

commit v1 on v0

v1 whole, which is shorter than its diff:
```python
import jax
import jax.numpy as jnp
from jax import lax
from jax.experimental import pallas as pl
from jax.experimental.pallas import tpu as pltpu
from jax.sharding import PartitionSpec as P

CX = 256

diffusion = 1.5
drift = 0.8
shear = 0.6
first_weights = (5.0 / 24.0, 1.0 / 3.0, -1.0 / 24.0)
second_weights = (-1.0 / 24.0, 1.0 / 3.0, 5.0 / 24.0)
whole_weights = (1.0 / 6.0, 2.0 / 3.0, 1.0 / 6.0)

MESH = pl.DeviceIdType.MESH
HALO = 8
BLOCK = 32
LANES = 128


def weighted(weights, fields):
    return [sum(w * f[k] for w, f in zip(weights, fields)) for k in range(2)]


def times(real, imag, field):
    return [real * field[0] - imag * field[1], real * field[1] + imag * field[0]]


def coupled(factor, field):
    length = field[0].shape[0]
    sums = [pltpu.roll(f, 1, 0) + pltpu.roll(f, length - 1, 0) for f in field]
    return [factor * sums[1], -factor * sums[0]]


def kernel(
    begin_hbm,
    nodes_hbm,
    start_out,
    nodes_out,
    ext,
    gain,
    shift,
    load_sem,
    start_sem,
    halo_send,
    halo_recv,
    bulk_send,
    bulk_recv,
    relay_send,
    relay_recv,
):
    slab, columns = begin_hbm.shape[1:]
    peers, count = lax.axis_size("space"), lax.axis_size("tm")
    total = slab * peers
    tm, rank = lax.axis_index("tm"), lax.axis_index("space")
    has_prev, has_next = tm > 0, tm < count - 1
    has_up, has_down = rank > 0, rank < peers - 1
    blocks = slab // BLOCK
    low_row = total // 2 - CX // 2
    low_column = columns // 2 - CX // 2
    coarse_rows = gain.shape[1]
    coarse_blocks = coarse_rows // BLOCK
    coarse_rank = (rank * slab < low_row + CX) & (rank * slab + slab > low_row)
    lower = rank < peers // 2
    coarse_start = jnp.clip(low_row - rank * slab, 0, slab - coarse_rows)
    coarse_block = coarse_start // BLOCK
    first = jnp.where(
        coarse_rank,
        jnp.where(lower, coarse_block, blocks - coarse_block - coarse_blocks),
        0,
    )

    def mirrored(index):
        return jnp.where(lower, index, blocks - 1 - index)

    def block_of(step):
        return mirrored(jnp.where(step < blocks - first, first + step, blocks - 1 - step))

    def load_of(step):
        later = jnp.where(step <= blocks - first, first + step - 1, blocks - 1 - step)
        early = jnp.where(step == 2, first - 1, first + step)
        moved = jnp.where(step <= 2, early, later)
        return mirrored(jnp.where(first == 0, step, moved))

    def rows_of(block):
        return pl.ds(pl.multiple_of(block * BLOCK, BLOCK), BLOCK)

    def loads(step):
        block = load_of(step)
        source = rows_of(block)
        target = pl.ds(pl.multiple_of(block * BLOCK + HALO, HALO), BLOCK)
        return (
            pltpu.make_async_copy(
                begin_hbm.at[:, source, :], ext.at[0, :, target, :], load_sem.at[0, step]
            ),
            pltpu.make_async_copy(
                nodes_hbm.at[:, :, source, :],
                ext.at[1:3, :, target, :],
                load_sem.at[1, step],
            ),
        )

    def halos(side):
        source = pl.ds(0 if side == 0 else slab - HALO, HALO)
        target = pl.ds(slab + HALO if side == 0 else 0, HALO)
        there = {"space": rank - 1 if side == 0 else rank + 1}
        return (
            pltpu.make_async_remote_copy(
                begin_hbm.at[:, source, :],
                ext.at[0, :, target, :],
                halo_send.at[0, side],
                halo_recv.at[0, side],
                device_id=there,
                device_id_type=MESH,
            ),
            pltpu.make_async_remote_copy(
                nodes_hbm.at[:, :, source, :],
                ext.at[1:3, :, target, :],
                halo_send.at[1, side],
                halo_recv.at[1, side],
                device_id=there,
                device_id_type=MESH,
            ),
        )

    following = {"tm": tm + 1}

    def relay_copy(step):
        place = (slice(None), rows_of(block_of(step)), pl.ds(low_column, CX))
        return pltpu.make_async_remote_copy(
            nodes_out.at[(1,) + place],
            start_out.at[place],
            relay_send.at[step],
            relay_recv.at[step],
            device_id=following,
            device_id_type=MESH,
        )

    def bulk(unit, act):
        step, half = unit // 2, unit % 2
        rows = rows_of(block_of(step))
        strip = coarse_rank & (step < coarse_blocks)

        def copy(place):
            return pltpu.make_async_remote_copy(
                nodes_out.at[(1,) + place],
                start_out.at[place],
                bulk_send.at[unit],
                bulk_recv.at[unit],
                device_id=following,
                device_id_type=MESH,
            )

        @pl.when(strip)
        def _():
            left = pl.multiple_of(half * (low_column + CX), LANES)
            act(copy((slice(None), rows, pl.ds(left, low_column))))

        @pl.when(jnp.logical_not(strip))
        def _():
            act(copy((half, rows, slice(None))))

    def send(low, high):
        @pl.when(has_next)
        def _():
            @pl.loop(low, high)
            def _(unit):
                bulk(unit, lambda c: c.start())

    whole_start = pltpu.make_async_copy(begin_hbm, start_out, start_sem)

    @pl.loop(0, blocks)
    def _(step):
        for c in loads(step):
            c.start()

    barrier = pltpu.get_barrier_semaphore()
    for there, exists in (
        ({"space": rank - 1}, has_up),
        ({"space": rank + 1}, has_down),
        ({"tm": tm - 1}, has_prev),
        ({"tm": tm + 1}, has_next),
    ):

        @pl.when(exists)
        def _(there=there):
            pl.semaphore_signal(barrier, inc=1, device_id=there, device_id_type=MESH)

    friends = sum(jnp.where(e, 1, 0) for e in (has_up, has_down, has_prev, has_next))
    pl.semaphore_wait(barrier, friends)

    for side, exists in ((0, has_up), (1, has_down)):

        @pl.when(exists)
        def _(side=side):
            for c in halos(side):
                c.start()

        @pl.when(jnp.logical_not(exists))
        def _(side=side):
            edge = pl.ds(0 if side == 0 else slab + HALO, HALO)
            ext[:, :, edge, :] = jnp.zeros((3, 2, HALO, columns), jnp.float32)

    @pl.when(jnp.logical_not(has_prev))
    def _():
        whole_start.start()

    def strip_compute(block, column, coarse):
        length = BLOCK + 2 * HALO
        span = pl.ds(pl.multiple_of(block * BLOCK, BLOCK), length)
        here = pl.ds(column, LANES)
        begin, one, two = [[ext[f, k, span, here] for k in range(2)] for f in range(3)]
        row = lax.broadcasted_iota(jnp.int32, (length, LANES), 0)
        row = row + (rank * slab + block * BLOCK - HALO)
        along = (row - total // 2).astype(jnp.float32) / (total // 2)
        place = lax.broadcasted_iota(jnp.int32, (1, LANES), 1) + column
        across = (place - columns // 2).astype(jnp.float32) / (columns // 2)
        inside = jnp.where((row >= 0) & (row < total), 1.0, 0.0).astype(jnp.float32)
        real = -diffusion * (along * along + across * across)
        imag = -drift * across
        factor = shear * across
        half_real, half_imag = 1.0 - 0.5 * real, -0.5 * imag
        scale = 1.0 / (half_real * half_real + half_imag * half_imag)
        inverse = (half_real * scale, -half_imag * scale)
        sum_one = weighted(first_weights, (begin, one, two))
        sum_two = weighted(second_weights, (begin, one, two))
        moved = times(real, imag, [s - 0.5 * o for s, o in zip(sum_one, one)])
        turned = coupled(factor, sum_one)
        inner = [begin[k] + moved[k] + turned[k] for k in range(2)]
        node_one = [inside * f for f in times(*inverse, inner)]
        moved = times(real, imag, [s - 0.5 * o for s, o in zip(sum_two, two)])
        turned = coupled(
            factor, [sum_two[k] + 0.5 * (node_one[k] - one[k]) for k in range(2)]
        )
        inner = [node_one[k] + moved[k] + turned[k] for k in range(2)]
        node_two = times(*inverse, inner)
        own = slice(HALO, HALO + BLOCK)
        rows = rows_of(block)
        if not coarse:
            for k in range(2):
                nodes_out[0, k, rows, here] = node_one[k][own]
                nodes_out[1, k, rows, here] = node_two[k][own]
            return
        mean = weighted(whole_weights, (begin, node_one, node_two))
        moved = times(real, imag, [mean[k] - node_two[k] for k in range(2)])
        turned = coupled(factor, mean)
        offset = [moved[k] + turned[k] for k in range(2)]
        step_real, step_imag = 1.0 - real, -imag
        scale = 1.0 / (step_real * step_real + step_imag * step_imag)
        grown = (step_real * scale, -step_imag * scale)
        offset = times(*grown, offset)
        local = pl.ds(pl.multiple_of(block * BLOCK - coarse_start, BLOCK), BLOCK)
        inner_here = pl.ds(pl.multiple_of(column - low_column, LANES), LANES)
        for k in range(2):
            gain[k, local, inner_here] = grown[k][own]
            shift[k, local, inner_here] = offset[k][own]
            kept = node_one[k] - 0.5 * (begin[k] + node_two[k])
            nodes_out[0, k, rows, here] = kept[own]

    def compute(step):
        block = block_of(step)
        arrived = jnp.where(step == 0, 0, step + 2)

        @pl.loop(arrived, jnp.minimum(step + 3, blocks))
        def _(which):
            for c in loads(which):
                c.wait()

        @pl.when((block == blocks - 1) & has_down)
        def _():
            for c in halos(0):
                c.wait_recv()

        @pl.when((block == 0) & has_up)
        def _():
            for c in halos(1):
                c.wait_recv()

        in_coarse = coarse_rank & (step < coarse_blocks)

        @pl.loop(0, columns // LANES)
        def _(index):
            column = pl.multiple_of(index * LANES, LANES)
            low = index * LANES
            coarse = in_coarse & (low >= low_column) & (low < low_column + CX)

            @pl.when(coarse)
            def _():
                strip_compute(block, column, True)

            @pl.when(jnp.logical_not(coarse))
            def _():
                strip_compute(block, column, False)

    def relay():
        @pl.when(jnp.logical_not(has_prev))
        def _():
            whole_start.wait()

        @pl.loop(0, coarse_blocks)
        def _(step):
            @pl.when(has_prev)
            def _():
                relay_copy(step).wait_recv()

            block = block_of(step)
            rows = rows_of(block)
            local = pl.ds(pl.multiple_of(block * BLOCK - coarse_start, BLOCK), BLOCK)
            here = pl.ds(low_column, CX)
            begin = [start_out[k, rows, here] for k in range(2)]
            grown = times(gain[0, local, :], gain[1, local, :], begin)
            finish = [grown[k] + shift[k, local, :] for k in range(2)]
            for k in range(2):
                nodes_out[1, k, rows, here] = finish[k]

            @pl.when(has_next)
            def _():
                relay_copy(step).start()

            for k in range(2):
                nodes_out[0, k, rows, here] += 0.5 * (begin[k] + finish[k])

    units = 2 * blocks
    waiting = jnp.minimum((3 * tm) // 2, units)
    opening = jnp.where(has_prev, jnp.minimum(waiting, 2 * coarse_blocks), 2 * coarse_blocks)
    middle = jnp.maximum(waiting, opening)

    @pl.when(coarse_rank)
    def _():
        @pl.loop(0, coarse_blocks)
        def _(step):
            compute(step)

        @pl.when(jnp.logical_not(has_prev))
        def _():
            relay()

        send(0, opening)

        @pl.loop(coarse_blocks, blocks)
        def _(step):
            compute(step)

        send(opening, middle)

        @pl.when(has_prev)
        def _():
            relay()

        send(middle, units)

    @pl.when(jnp.logical_not(coarse_rank))
    def _():
        @pl.loop(0, blocks)
        def _(step):
            compute(step)
            send(2 * step, 2 * step + 2)

        @pl.when(jnp.logical_not(has_prev))
        def _():
            whole_start.wait()

    for side, exists in ((0, has_up), (1, has_down)):

        @pl.when(exists)
        def _(side=side):
            for c in halos(side):
                c.wait_send()

    @pl.when(coarse_rank & has_next)
    def _():
        @pl.loop(0, coarse_blocks)
        def _(step):
            relay_copy(step).wait_send()

    @pl.when(has_prev)
    def _():
        @pl.loop(0, units)
        def _(unit):
            bulk(unit, lambda c: c.wait_recv())

    @pl.when(has_next)
    def _():
        @pl.loop(0, units)
        def _(unit):
            bulk(unit, lambda c: c.wait_send())


def body(start_values, node_values):
    slab, columns = start_values.shape[2:]
    peers = lax.axis_size("space")
    coarse_rows = min(slab, max(CX // 2, CX // peers))
    blocks, coarse_blocks = slab // BLOCK, coarse_rows // BLOCK
    hbm = pl.BlockSpec(memory_space=pltpu.HBM)
    vmem = pl.BlockSpec(memory_space=pltpu.VMEM)
    dma = pltpu.SemaphoreType.DMA
    start, nodes = pl.pallas_call(
        kernel,
        out_shape=(
            OUT((2, slab, columns), jnp.float32),
            OUT((2, 2, slab, columns), jnp.float32),
        ),
        in_specs=[hbm, hbm],
        out_specs=(vmem, vmem),
        scratch_shapes=[
            pltpu.VMEM((3, 2, slab + 2 * HALO, columns), jnp.float32),
            pltpu.VMEM((2, coarse_rows, CX), jnp.float32),
            pltpu.VMEM((2, coarse_rows, CX), jnp.float32),
            dma((2, blocks)),
            dma,
            dma((2, 2)),
            dma((2, 2)),
            dma((2 * blocks,)),
            dma((2 * blocks,)),
            dma((coarse_blocks,)),
            dma((coarse_blocks,)),
        ],
        compiler_params=pltpu.CompilerParams(
            collective_id=0, has_side_effects=True, vmem_limit_bytes=56 * 1024 * 1024
        ),
    )(start_values[0], node_values[0])
    return (start[None], nodes[None])


OUT = pltpu.VMEM


def solution(mesh):
    in_specs = (P("tm", None, "space", None), P("tm", None, None, "space", None))
    out_specs = (P("tm", None, "space", None), P("tm", None, None, "space", None))
    return jax.shard_map(body, mesh=mesh, in_specs=in_specs, out_specs=out_specs, check_vma=False)
```

time: 235 us -> 55.3 us (0.24)
  the two profiles are of different devices: /device:TPU:8 before, /device:TPU:9 now
where the time goes in v1:
time: 55.3 us; the launch traced here: 55.1 us
  Pallas kernels  51.2 us (93%)
  local copies, waits for them, and re-layouts  3.33 us (6%)
  between operations  0.64 us (1%)
    pallas_call x1, Pallas kernels, body(): pl.pallas_call(kernel, out_shape=(OUT((2, slab, columns), jnp.float32), O...  51.2 us
    unnamed x2, local copies, waits for them, and re-layouts  3.33 us

profile of v1, /device:TPU:9, one launch (start us, length us, event | category | flops | bytes accessed | tf_op | source)
XLA Modules:
  0.0 55.1 jit_solution(14239343071774089173)
XLA Ops:
  0.6 51.2 %shard_map.41 = (f32[2,256,1024]{2,1,0:T(8,128)S(1)}, f32[2,2,256,1024]{3,2,1,0:T(8,128)S(1)}) custom-call(f32[2,256,1024]{2,1,0:T(8,128)} %bitcast.7, f32[2,2,256,1024]{3,2,1,0:T(8,128)} %bitcast.6), custom_call_target="tpu_custom_call" | custom-call | tf_op jit(solution)/shard_map/pallas_call | solution.py:399
  51.8 1.3 %copy.6 = f32[1,2,256,1024]{3,2,1,0:T(8,128)} copy(f32[1,2,256,1024]{3,2,1,0:T(8,128)S(1)} %bitcast.5) | data formatting | bytes 4194304
  53.1 2.0 %copy.7 = f32[1,2,2,256,1024]{4,3,2,1,0:T(8,128)} copy(f32[1,2,2,256,1024]{4,3,2,1,0:T(8,128)S(1)} %bitcast.4) | data formatting | bytes 8388608

commit v2 on v1

--- a/solution.py
+++ b/solution.py
@@ -17,6 +17,7 @@
 MESH = pl.DeviceIdType.MESH
 HALO = 8
 BLOCK = 32
+PARTS = 4
 LANES = 128
 
 
@@ -139,8 +140,8 @@
         )
 
     def bulk(unit, act):
-        step, half = unit // 2, unit % 2
-        rows = rows_of(block_of(step))
+        step, part = unit // PARTS, unit % PARTS
+        block = block_of(step)
         strip = coarse_rank & (step < coarse_blocks)
 
         def copy(place):
@@ -155,12 +156,16 @@
 
         @pl.when(strip)
         def _():
-            left = pl.multiple_of(half * (low_column + CX), LANES)
-            act(copy((slice(None), rows, pl.ds(left, low_column))))
+            height = 2 * BLOCK // PARTS
+            top = pl.multiple_of(block * BLOCK + (part // 2) * height, HALO)
+            left = pl.multiple_of((part % 2) * (low_column + CX), LANES)
+            act(copy((slice(None), pl.ds(top, height), pl.ds(left, low_column))))
 
         @pl.when(jnp.logical_not(strip))
         def _():
-            act(copy((half, rows, slice(None))))
+            width = columns // PARTS
+            left = pl.multiple_of(part * width, LANES)
+            act(copy((slice(None), rows_of(block), pl.ds(left, width))))
 
     def send(low, high):
         @pl.when(has_next)
@@ -170,11 +175,6 @@
                 bulk(unit, lambda c: c.start())
 
     whole_start = pltpu.make_async_copy(begin_hbm, start_out, start_sem)
-
-    @pl.loop(0, blocks)
-    def _(step):
-        for c in loads(step):
-            c.start()
 
     barrier = pltpu.get_barrier_semaphore()
     for there, exists in (
@@ -188,15 +188,12 @@
         def _(there=there):
             pl.semaphore_signal(barrier, inc=1, device_id=there, device_id_type=MESH)
 
-    friends = sum(jnp.where(e, 1, 0) for e in (has_up, has_down, has_prev, has_next))
-    pl.semaphore_wait(barrier, friends)
+    @pl.loop(0, blocks)
+    def _(step):
+        for c in loads(step):
+            c.start()
 
     for side, exists in ((0, has_up), (1, has_down)):
-
-        @pl.when(exists)
-        def _(side=side):
-            for c in halos(side):
-                c.start()
 
         @pl.when(jnp.logical_not(exists))
         def _(side=side):
@@ -206,6 +203,16 @@
     @pl.when(jnp.logical_not(has_prev))
     def _():
         whole_start.start()
+
+    def greet():
+        friends = sum(jnp.where(e, 1, 0) for e in (has_up, has_down, has_prev, has_next))
+        pl.semaphore_wait(barrier, friends)
+        for side, exists in ((0, has_up), (1, has_down)):
+
+            @pl.when(exists)
+            def _(side=side):
+                for c in halos(side):
+                    c.start()
 
     def strip_compute(block, column, coarse):
         length = BLOCK + 2 * HALO
@@ -259,11 +266,13 @@
             kept = node_one[k] - 0.5 * (begin[k] + node_two[k])
             nodes_out[0, k, rows, here] = kept[own]
 
-    def compute(step):
+    lead = jnp.where(first == 0, 2, 3)
+
+    def compute(step, after=None):
         block = block_of(step)
-        arrived = jnp.where(step == 0, 0, step + 2)
-
-        @pl.loop(arrived, jnp.minimum(step + 3, blocks))
+        arrived = jnp.where(step == 0, 0, step + lead - 1)
+
+        @pl.loop(arrived, jnp.minimum(step + lead, blocks))
         def _(which):
             for c in loads(which):
                 c.wait()
@@ -279,20 +288,29 @@
                 c.wait_recv()
 
         in_coarse = coarse_rank & (step < coarse_blocks)
-
-        @pl.loop(0, columns // LANES)
-        def _(index):
-            column = pl.multiple_of(index * LANES, LANES)
-            low = index * LANES
-            coarse = in_coarse & (low >= low_column) & (low < low_column + CX)
-
-            @pl.when(coarse)
-            def _():
-                strip_compute(block, column, True)
-
-            @pl.when(jnp.logical_not(coarse))
-            def _():
-                strip_compute(block, column, False)
+        strips = columns // LANES // PARTS
+
+        @pl.loop(0, PARTS)
+        def _(part):
+            @pl.loop(0, strips)
+            def _(index):
+                low = (part * strips + index) * LANES
+                column = pl.multiple_of(low, LANES)
+                if after is not None:
+                    strip_compute(block, column, False)
+                    return
+                coarse = in_coarse & (low >= low_column) & (low < low_column + CX)
+
+                @pl.when(coarse)
+                def _():
+                    strip_compute(block, column, True)
+
+                @pl.when(jnp.logical_not(coarse))
+                def _():
+                    strip_compute(block, column, False)
+
+            if after is not None:
+                after(PARTS * step + part)
 
     def relay():
         @pl.when(jnp.logical_not(has_prev))
@@ -322,13 +340,15 @@
             for k in range(2):
                 nodes_out[0, k, rows, here] += 0.5 * (begin[k] + finish[k])
 
-    units = 2 * blocks
-    waiting = jnp.minimum((3 * tm) // 2, units)
-    opening = jnp.where(has_prev, jnp.minimum(waiting, 2 * coarse_blocks), 2 * coarse_blocks)
+    units = PARTS * blocks
+    waiting = jnp.minimum((3 * PARTS * tm) // 4, units)
+    opening = jnp.where(has_prev, jnp.minimum(waiting, PARTS * coarse_blocks), PARTS * coarse_blocks)
     middle = jnp.maximum(waiting, opening)
 
     @pl.when(coarse_rank)
     def _():
+        greet()
+
         @pl.loop(0, coarse_blocks)
         def _(step):
             compute(step)
@@ -353,10 +373,16 @@
 
     @pl.when(jnp.logical_not(coarse_rank))
     def _():
+        def after(unit):
+            @pl.when(unit == 0)
+            def _():
+                greet()
+
+            send(unit, unit + 1)
+
         @pl.loop(0, blocks)
         def _(step):
-            compute(step)
-            send(2 * step, 2 * step + 2)
+            compute(step, after)
 
         @pl.when(jnp.logical_not(has_prev))
         def _():
@@ -386,6 +412,19 @@
         @pl.loop(0, units)
         def _(unit):
             bulk(unit, lambda c: c.wait_send())
+
+
+def write_out(start, nodes, start_hbm, nodes_hbm, sem):
+    copies = [
+        pltpu.make_async_copy(nodes.at[f, k], nodes_hbm.at[f, k], sem.at[2 * f + k])
+        for f in range(2)
+        for k in range(2)
+    ]
+    copies += [pltpu.make_async_copy(start.at[k], start_hbm.at[k], sem.at[4 + k]) for k in range(2)]
+    for c in copies:
+        c.start()
+    for c in copies:
+        c.wait()
 
 
 def body(start_values, node_values):
@@ -412,8 +451,8 @@
             dma,
             dma((2, 2)),
             dma((2, 2)),
-            dma((2 * blocks,)),
-            dma((2 * blocks,)),
+            dma((PARTS * blocks,)),
+            dma((PARTS * blocks,)),
             dma((coarse_blocks,)),
             dma((coarse_blocks,)),
         ],
@@ -421,6 +460,17 @@
             collective_id=0, has_side_effects=True, vmem_limit_bytes=56 * 1024 * 1024
         ),
     )(start_values[0], node_values[0])
+    start, nodes = pl.pallas_call(
+        write_out,
+        out_shape=(
+            jax.ShapeDtypeStruct(start.shape, jnp.float32),
+            jax.ShapeDtypeStruct(nodes.shape, jnp.float32),
+        ),
+        in_specs=[pl.BlockSpec(memory_space=pl.ANY)] * 2,
+        out_specs=(hbm, hbm),
+        scratch_shapes=[dma((6,))],
+        compiler_params=pltpu.CompilerParams(vmem_limit_bytes=2 * 1024 * 1024),
+    )(start, nodes)
     return (start[None], nodes[None])
 
 

time: 55.3 us -> 54.2 us (0.980)
  local copies, waits for them, and re-layouts: 3.33 us -> 0 us
  Pallas kernels: 51.2 us -> 53.4 us
    unnamed x2 -> x0, local copies, waits for them, and re-layouts: 3.33 us -> none
    pallas_call x0 -> x1, Pallas kernels: none -> 2.72 us  [body(): pl.pallas_call(write_out, out_shape=(jax.ShapeDtypeStruct(start.shape, jn...]
where the time goes in v2:
time: 54.2 us; the launch traced here: 54.1 us
  Pallas kernels  53.4 us (99%)
  between operations  0.64 us (1%)
    pallas_call x1, Pallas kernels, body(): pl.pallas_call(kernel, out_shape=(OUT((2, slab, columns), jnp.float32), O...  50.7 us
    pallas_call x1, Pallas kernels, body(): pl.pallas_call(write_out, out_shape=(jax.ShapeDtypeStruct(start.shape, jn...  2.72 us

profile of v2, /device:TPU:9, one launch (start us, length us, event | category | flops | bytes accessed | tf_op | source)
XLA Modules:
  0.0 54.1 jit_solution(9997817544628587584)
XLA Ops:
  0.6 50.7 %shard_map.41 = (f32[2,256,1024]{2,1,0:T(8,128)S(1)}, f32[2,2,256,1024]{3,2,1,0:T(8,128)S(1)}) custom-call(f32[2,256,1024]{2,1,0:T(8,128)} %bitcast.5, f32[2,2,256,1024]{3,2,1,0:T(8,128)} %bitcast.4), custom_call_target="tpu_custom_call" | custom-call | tf_op jit(solution)/shard_map/pallas_call | solution.py:438
  51.4 2.7 %shard_map.42 = (f32[2,256,1024]{2,1,0:T(8,128)}, f32[2,2,256,1024]{3,2,1,0:T(8,128)}) custom-call(f32[2,256,1024]{2,1,0:T(8,128)S(1)} %get-tuple-element.6.start, f32[2,2,256,1024]{3,2,1,0:T(8,128)S(1)} %get-tuple-element.7.nodes), custom_call_target="tpu_custom_call" | custom-call | tf_op jit(solution)/shard_map/pallas_call | solution.py:463

commit v3 on v2

--- a/solution.py
+++ b/solution.py
@@ -18,6 +18,8 @@
 HALO = 8
 BLOCK = 32
 PARTS = 4
+STRIPS = 2
+WHOLES = 1
 LANES = 128
 
 
@@ -154,17 +156,25 @@
                 device_id_type=MESH,
             )
 
-        @pl.when(strip)
-        def _():
-            height = 2 * BLOCK // PARTS
-            top = pl.multiple_of(block * BLOCK + (part // 2) * height, HALO)
+        @pl.when(strip & (part >= PARTS - STRIPS))
+        def _():
+            height = 2 * BLOCK // STRIPS
+            top = pl.multiple_of(block * BLOCK + (part - (PARTS - STRIPS)) // 2 * height, HALO)
             left = pl.multiple_of((part % 2) * (low_column + CX), LANES)
             act(copy((slice(None), pl.ds(top, height), pl.ds(left, low_column))))
 
-        @pl.when(jnp.logical_not(strip))
+        quick = (step == 0) & jnp.logical_not(coarse_rank)
+
+        @pl.when(quick)
         def _():
             width = columns // PARTS
             left = pl.multiple_of(part * width, LANES)
+            act(copy((slice(None), rows_of(block), pl.ds(left, width))))
+
+        @pl.when(jnp.logical_not(quick | strip) & ((part + 1) % (PARTS // WHOLES) == 0))
+        def _():
+            width = columns // WHOLES
+            left = pl.multiple_of(part // (PARTS // WHOLES) * width, LANES)
             act(copy((slice(None), rows_of(block), pl.ds(left, width))))
 
     def send(low, high):
@@ -341,7 +351,7 @@
                 nodes_out[0, k, rows, here] += 0.5 * (begin[k] + finish[k])
 
     units = PARTS * blocks
-    waiting = jnp.minimum((3 * PARTS * tm) // 4, units)
+    waiting = jnp.minimum(PARTS * tm // 2, units)
     opening = jnp.where(has_prev, jnp.minimum(waiting, PARTS * coarse_blocks), PARTS * coarse_blocks)
     middle = jnp.maximum(waiting, opening)
 

time: 54.2 us -> 54.2 us (level)
  no operation moved by 1% of the time
where the time goes in v3:
time: 54.2 us; the launch traced here: 54 us
  Pallas kernels  53.4 us (99%)
  between operations  0.64 us (1%)
    pallas_call x1, Pallas kernels, body(): pl.pallas_call(kernel, out_shape=(OUT((2, slab, columns), jnp.float32), O...  50.7 us
    pallas_call x1, Pallas kernels, body(): pl.pallas_call(write_out, out_shape=(jax.ShapeDtypeStruct(start.shape, jn...  2.72 us

profile of v3, /device:TPU:9, one launch (start us, length us, event | category | flops | bytes accessed | tf_op | source)
XLA Modules:
  0.0 54.0 jit_solution(6222111837623256092)
XLA Ops:
  0.6 50.7 %shard_map.41 = (f32[2,256,1024]{2,1,0:T(8,128)S(1)}, f32[2,2,256,1024]{3,2,1,0:T(8,128)S(1)}) custom-call(f32[2,256,1024]{2,1,0:T(8,128)} %bitcast.5, f32[2,2,256,1024]{3,2,1,0:T(8,128)} %bitcast.4), custom_call_target="tpu_custom_call" | custom-call | tf_op jit(solution)/shard_map/pallas_call | solution.py:448
  51.3 2.7 %shard_map.42 = (f32[2,256,1024]{2,1,0:T(8,128)}, f32[2,2,256,1024]{3,2,1,0:T(8,128)}) custom-call(f32[2,256,1024]{2,1,0:T(8,128)S(1)} %get-tuple-element.6.start, f32[2,2,256,1024]{3,2,1,0:T(8,128)S(1)} %get-tuple-element.7.nodes), custom_call_target="tpu_custom_call" | custom-call | tf_op jit(solution)/shard_map/pallas_call | solution.py:473
